TPU v7x, 32 devices: a whole 2x2x4 slice. The times are simulated.
32 devices in a mesh: dp: 8 (over y, x, core), tensor: 4 (over z).
Axes of the slice: x: 2, y: 2, z: 4, core: 2. Of those that a mesh axis runs over, the one named last changes fastest.
Arguments:
- tokens: bfloat16 [8192, 1024], P(('dp', 'tensor')), may hold values from -6 to 6
- upstream: bfloat16 [8192, 1024], P(('dp', 'tensor')), may hold values from -6 to 6
- counts: int32 [128], P('dp'), may hold values from 37 to 49, as said below
- norm_gain: float32 [1024], replicated, may hold values from 0.5 to 1.5
- norm_bias: float32 [1024], replicated, may hold values from -4 to 4
- w_qkv: bfloat16 [1024, 3072], P('dp', 'tensor'), may hold values from -0.1875 to 0.1875
- w_out: bfloat16 [1024, 1024], P('tensor', 'dp'), may hold values from -0.1875 to 0.1875
Outputs:
- grad_tokens: bfloat16 [8192, 1024], P(('dp', 'tensor'))
- grad_qkv: float32 [1024, 3072], P('dp', 'tensor')
- grad_out: float32 [1024, 1024], P('tensor', 'dp')
- grad_gain: float32 [1024], replicated
- grad_bias: float32 [1024], replicated
Inputs may be any that keep to these rules, and one draw needn't show every extreme that they name: counts[i] is the number of visible tokens of image i, held in its first slots; some image has 49 in every draw.
All inputs are finite; a program needn't handle non-finite values.
Results may differ from a plain program's by a relative error of at most 0.014.
Values may be sent and summed in bfloat16 or wider, within the bound.
A program may use at most 64 MiB of HBM per device.

v0:
```python
import jax
import jax.numpy as jnp
from jax import lax
from jax.sharding import PartitionSpec as P

HEAD = 64
CAP = 64


def layer_norm(tokens, norm_gain, norm_bias):
    values = tokens.astype(jnp.float32)
    centre = jnp.mean(values, axis=-1, keepdims=True)
    shifted = values - centre
    variance = jnp.mean(shifted * shifted, axis=-1, keepdims=True)
    inverse_std = lax.rsqrt(variance + 1e-06)
    scaled = shifted * inverse_std
    normed = (scaled * norm_gain + norm_bias).astype(jnp.bfloat16)
    return (normed, scaled, inverse_std)


def on_device(tokens, upstream, counts, norm_gain, norm_bias, w_qkv, w_out):
    local_rows = tokens.shape[0]
    own_images = local_rows // CAP
    start_image = lax.axis_index("tensor") * own_images
    own_counts = lax.dynamic_slice_in_dim(counts, start_image, own_images)
    own_live = (
        (jnp.arange(CAP, dtype=jnp.int32)[None, :] < own_counts[:, None])
        .reshape(-1)
        .astype(jnp.float32)
    )
    normed, scaled, inverse_std = layer_norm(tokens, norm_gain, norm_bias)
    all_normed = lax.all_gather(normed, "tensor", axis=0, tiled=True)
    qkv_cols = lax.all_gather(w_qkv, "dp", axis=0, tiled=True)
    out_rows = lax.all_gather(w_out, "dp", axis=1, tiled=True)
    all_upstream = lax.all_gather(upstream, "tensor", axis=0, tiled=True)
    group_rows = all_normed.shape[0]
    images = group_rows // CAP
    local_heads = qkv_cols.shape[1] // (3 * HEAD)
    slot_live = jnp.arange(CAP, dtype=jnp.int32)[None, :] < counts[:, None]
    group_live = slot_live.reshape(-1).astype(jnp.bfloat16)
    masked = all_upstream * group_live[:, None]
    projected = jnp.dot(all_normed, qkv_cols, preferred_element_type=jnp.float32).astype(
        jnp.bfloat16
    )
    projected = projected.reshape(images, CAP, local_heads, 3, HEAD)
    query_rows = projected[:, :, :, 0]
    key_rows = projected[:, :, :, 1]
    value_rows = projected[:, :, :, 2]
    score_scale = 1.0 / HEAD**0.5
    scores = (
        jnp.einsum("bqhe,bkhe->bhqk", query_rows, key_rows, preferred_element_type=jnp.float32)
        * score_scale
    )
    scores = jnp.where(slot_live[:, None, None, :], scores, -1e30)
    probs = jax.nn.softmax(scores, axis=-1)
    probs_low = probs.astype(jnp.bfloat16)
    attended = jnp.einsum(
        "bhqk,bkhe->bqhe", probs_low, value_rows, preferred_element_type=jnp.float32
    )
    attended = attended.astype(jnp.bfloat16).reshape(group_rows, local_heads * HEAD)
    out_part = lax.dot_general(
        attended, masked, (((0,), (0,)), ((), ())), preferred_element_type=jnp.float32
    )
    grad_out = lax.psum_scatter(
        out_part.astype(jnp.bfloat16), "dp", scatter_dimension=1, tiled=True
    ).astype(jnp.float32)
    grad_att = lax.dot_general(
        masked, out_rows, (((1,), (1,)), ((), ())), preferred_element_type=jnp.float32
    )
    grad_att = grad_att.astype(jnp.bfloat16).reshape(images, CAP, local_heads, HEAD)
    grad_probs = jnp.einsum(
        "bqhe,bkhe->bhqk", grad_att, value_rows, preferred_element_type=jnp.float32
    )
    row_delta = jnp.sum(probs * grad_probs, axis=-1, keepdims=True)
    grad_scores = (probs * (grad_probs - row_delta) * score_scale).astype(jnp.bfloat16)
    grad_value = jnp.einsum(
        "bhqk,bqhe->bkhe", probs_low, grad_att, preferred_element_type=jnp.float32
    ).astype(jnp.bfloat16)
    grad_query = jnp.einsum(
        "bhqk,bkhe->bqhe", grad_scores, key_rows, preferred_element_type=jnp.float32
    ).astype(jnp.bfloat16)
    grad_key = jnp.einsum(
        "bhqk,bqhe->bkhe", grad_scores, query_rows, preferred_element_type=jnp.float32
    ).astype(jnp.bfloat16)
    grad_proj = jnp.stack([grad_query, grad_key, grad_value], axis=3).reshape(
        group_rows, 3 * local_heads * HEAD
    )
    qkv_part = lax.dot_general(
        all_normed, grad_proj, (((0,), (0,)), ((), ())), preferred_element_type=jnp.float32
    )
    grad_qkv = lax.psum_scatter(
        qkv_part.astype(jnp.bfloat16), "dp", scatter_dimension=0, tiled=True
    ).astype(jnp.float32)
    grad_normed = lax.psum_scatter(
        lax.dot_general(
            grad_proj, qkv_cols, (((1,), (1,)), ((), ())), preferred_element_type=jnp.float32
        ).astype(jnp.bfloat16),
        "tensor",
        scatter_dimension=0,
        tiled=True,
    ).astype(jnp.float32)
    grad_gain, grad_bias = lax.psum(
        (jnp.sum(grad_normed * scaled, axis=0), jnp.sum(grad_normed, axis=0)), ("dp", "tensor")
    )
    grad_scaled = grad_normed * norm_gain
    grad_ln = inverse_std * (
        grad_scaled
        - jnp.mean(grad_scaled, axis=-1, keepdims=True)
        - scaled * jnp.mean(grad_scaled * scaled, axis=-1, keepdims=True)
    )
    grad_tokens = (upstream.astype(jnp.float32) * own_live[:, None] + grad_ln).astype(jnp.bfloat16)
    return (grad_tokens, grad_qkv, grad_out, grad_gain, grad_bias)


def solution(mesh):
    return jax.shard_map(
        on_device,
        mesh=mesh,
        in_specs=(
            P(("dp", "tensor"), None),
            P(("dp", "tensor"), None),
            P("dp"),
            P(),
            P(),
            P("dp", "tensor"),
            P("tensor", "dp"),
        ),
        out_specs=(P(("dp", "tensor"), None), P("dp", "tensor"), P("tensor", "dp"), P(), P()),
        check_vma=False,
    )
```

profile of v0, /device:TPU:0, one launch (start us, length us, event | category | flops | bytes accessed | tf_op | source)
XLA Modules:
  0.0 332.8 jit_solution(4929097271266516613)
XLA Ops:
  13.6 12.6 %all_gather.15 = bf16[256,1024]{1,0:T(8,128)(2,1)S(1)} all-gather(bf16[256,128]{1,0:T(8,128)(2,1)S(1)} %copy-done.6), channel_id=1, replica_groups=mesh['dp'=8,'tensor'=4] {'dp'}, dimensions={1}, use_global_device_ids=true | all-gather | bytes 589824 | tf_op jit(solution)/shard_map/all_gather | solution.py:34
  26.2 12.7 %all-gather.6.cloned.1.call-done = bf16[1024,768]{1,0:T(8,128)(2,1)} async-done(((bf16[128,768]{1,0:T(8,128)(2,1)}), bf16[1024,768]{1,0:T(8,128)(2,1)}) %all-gather.6.cloned.1.call-update) | async-done | bytes 1572880 | tf_op jit(solution)/shard_map/all_gather | solution.py:33
  38.9 47.8 %all-gather.4.cloned.1.call-done = bf16[1024,1024]{1,0:T(8,128)(2,1)} async-done(((bf16[256,1024]{1,0:T(8,128)(2,1)}), bf16[1024,1024]{1,0:T(8,128)(2,1)}) %all-gather.4.cloned.1.call-update) | async-done | bytes 2097168 | tf_op jit(solution)/shard_map/all_gather | solution.py:32
  86.7 3.8 %convolution_convert_fusion.2 = bf16[1024,768]{1,0:T(8,128)(2,1)S(1)} fusion(bf16[1024,1024]{1,0:T(8,128)(2,1)} %all-gather.4.cloned.1.call-done, bf16[1024,768]{1,0:T(8,128)(2,1)} %all-gather.6.cloned.1.call-done), kind=kOutput, calls=%fused_computation.15 | convolution fusion | flops 1611399168 | bytes 5242880 | tf_op jit(solution)/shard_map/dot_general | solution.py:42
  90.6 5.0 %reshape.105 = bf16[16,64,4,3,64]{4,3,2,1,0:T(4,128)(2,1)} reshape(bf16[1024,768]{1,0:T(8,128)(2,1)S(1)} %convolution_convert_fusion.2) | data formatting | bytes 3145728 | tf_op jit(solution)/shard_map/reshape | solution.py:45
  95.5 11.4 %fusion.71 = (bf16[16,64,4,1,64]{4,3,2,1,0:T(2,128)(2,1)S(1)}, bf16[16,64,4,1,64]{4,3,2,1,0:T(2,128)(2,1)}, bf16[16,64,4,1,64]{4,3,2,1,0:T(2,128)(2,1)}) fusion(bf16[16,64,4,3,64]{4,3,2,1,0:T(4,128)(2,1)} %reshape.105), kind=kLoop, calls=%fused_computation.78 | loop fusion | bytes 3145728 | tf_op jit(solution)/shard_map/slice | solution.py:48
  106.9 25.9 %all-gather.8.cloned.1.call-done = bf16[1024,1024]{1,0:T(8,128)(2,1)} async-done(((bf16[256,1024]{1,0:T(8,128)(2,1)}), bf16[1024,1024]{1,0:T(8,128)(2,1)}) %all-gather.8.cloned.1.call-update) | async-done | bytes 2097168 | tf_op jit(solution)/shard_map/all_gather | solution.py:35
  132.8 3.1 fusion.33
  139.3 2.9 fusion.62
  142.3 4.8 %fusion.72 = (f32[16,4,64]{2,1,0:T(4,128)S(1)}, f32[16,4,64,64]{2,3,1,0:T(8,128)}) fusion(pred[16,64]{1,0:T(8,128)(4,1)S(1)} %get-tuple-element.14, bf16[16,64,4,1,64]{4,3,2,1,0:T(2,128)(2,1)} %get-tuple-element.13, bf16[16,64,4,1,64]{4,3,2,1,0:T(2,128)(2,1)} %get-tuple-element.12), kind=kOutput, calls=%fused_computation.79 | convolution fusion | flops 34603072 | bytes 2114560 | tf_op jit(solution)/shard_map/sub | solution.py:55
  147.1 3.4 %fusion.25 = bf16[16,64,4,1,64]{1,4,2,0,3:T(8,128)(2,1)} fusion(bf16[16,64,4,64]{1,3,2,0:T(8,128)(2,1)S(1)} %copy-done.1, f32[16,4,64,64]{2,3,1,0:T(8,128)} %get-tuple-element.17, f32[16,4,64]{2,1,0:T(4,128)S(1)} %get-tuple-element.16), kind=kOutput, calls=%fused_computation.28 | convolution fusion | flops 34340864 | bytes 2113536 | tf_op jit(solution)/shard_map/bhqk,bqhe->bkhe/dot_general | solution.py:76
  151.0 6.1 %fusion.30 = bf16[16,64,4,1,64]{1,4,2,0,3:T(8,128)(2,1)} fusion(f32[16,4,64,64]{2,3,1,0:T(8,128)} %fusion.62, bf16[16,64,4,1,64]{4,3,2,1,0:T(2,128)(2,1)} %get-tuple-element.13, f32[16,4,64,64]{2,3,1,0:T(8,128)} %get-tuple-element.17, f32[16,4,64]{2,1,0:T(4,128)S(1)} %get-tuple-element.16), kind=kOutput, calls=%fused_computation.31 | convolution fusion | flops 35655744 | bytes 3162112 | tf_op jit(solution)/shard_map/bhqk,bkhe->bqhe/dot_general | solution.py:79
  158.5 2.5 fusion.36
  162.3 5.6 %fusion.27 = bf16[16,64,4,1,64]{1,4,2,0,3:T(8,128)(2,1)} fusion(f32[16,4,64,64]{2,3,1,0:T(8,128)} %fusion.62, bf16[16,64,4,1,64]{4,3,2,1,0:T(2,128)(2,1)S(1)} %copy-done.3, f32[16,4,64,64]{2,3,1,0:T(8,128)} %get-tuple-element.17, f32[16,4,64]{2,1,0:T(4,128)S(1)} %get-tuple-element.16), kind=kOutput, calls=%fused_computation.30 | convolution fusion | flops 35655744 | bytes 3162112 | tf_op jit(solution)/shard_map/bhqk,bqhe->bkhe/dot_general | solution.py:82
  167.9 2.3 pad_maximum_fusion
  170.2 2.4 copy.50
  172.7 3.2 reshape.99
  175.9 5.2 %convolution_convert_fusion.1 = bf16[1024,768]{1,0:T(8,128)(2,1)} fusion(bf16[1024,1024]{1,0:T(8,128)(2,1)} %all-gather.4.cloned.1.call-done, bf16[1024,768]{0,1:T(8,128)(2,1)} %reshape.99), kind=kOutput, calls=%fused_computation.14 | convolution fusion | flops 1611399168 | bytes 5242880 | tf_op jit(solution)/shard_map/dot_general | solution.py:88
  181.2 3.2 convolution_convert_fusion
  184.6 10.5 %reduce-scatter.10.cloned.1.call-done = bf16[128,256]{1,0:T(8,128)(2,1)} async-done(((bf16[1024,256]{1,0:T(8,128)(2,1)}), bf16[128,256]{1,0:T(8,128)(2,1)}) %reduce-scatter.10.cloned.1.call-update) | async-done | bytes 65552
  196.8 39.9 %reduce-scatter.8.cloned.1.call-done = bf16[128,768]{1,0:T(8,128)(2,1)} async-done(((bf16[1024,768]{1,0:T(8,128)(2,1)}), bf16[128,768]{1,0:T(8,128)(2,1)}) %reduce-scatter.8.cloned.1.call-update) | async-done | bytes 196624 | tf_op jit(solution)/shard_map/reduce_scatter | solution.py:91
  238.4 44.1 %reduce-scatter.6.cloned.1.call-done = bf16[256,1024]{1,0:T(8,128)(2,1)} async-done(((bf16[1024,1024]{1,0:T(8,128)(2,1)}), bf16[256,1024]{1,0:T(8,128)(2,1)}) %reduce-scatter.6.cloned.1.call-update) | async-done | bytes 524304 | tf_op jit(solution)/shard_map/reduce_scatter | solution.py:94
  284.1 39.5 %all-reduce = (f32[1024]{0:T(1024)}, f32[1024]{0:T(1024)}) all-reduce(f32[1024]{0:T(1024)S(1)} %get-tuple-element.5, f32[1024]{0:T(1024)S(1)} %get-tuple-element.8), channel_id=1, replica_groups=mesh['dp'=8,'tensor'=4] {'dp','tensor'}, use_global_device_ids=true, to_apply=%region_11.12 | all-reduce | flops 2048 | bytes 16384 | tf_op jit(solution)/shard_map/psum | solution.py:102
  323.6 2.3 fusion.48
  (55 shorter events, 18.2 us)
Async XLA Ops:
  7.2 6.3 %copy-start.8 = (s32[16]{0:T(128)S(1)}, s32[16]{0:T(128)}, u32[]{:S(2)}) copy-start(s32[16]{0:T(128)} %param.9) | copy-start | bytes 196
  7.2 6.4 %copy-start.6 = (bf16[256,128]{1,0:T(8,128)(2,1)S(1)}, bf16[256,128]{1,0:T(8,128)(2,1)}, u32[]{:S(2)}) copy-start(bf16[256,128]{1,0:T(8,128)(2,1)} %param.13) | copy-start | bytes 196612
  7.2 31.7 %all-gather.6.cloned.1.call-start = ((), (), s32[]{:S(2)}) async-start(), calls=%async_computation.4 | async-start | bytes 1769472 | tf_op jit(solution)/shard_map/all_gather | solution.py:33
  7.9 78.8 %all-gather.4.cloned.1.call-start = ((), (), s32[]{:S(2)}) async-start(), calls=%async_computation.3 | async-start | bytes 2621440 | tf_op jit(solution)/shard_map/all_gather | solution.py:32
  12.7 120.2 %all-gather.8.cloned.1.call-start = ((), (), s32[]{:S(2)}) async-start(), calls=%async_computation.5 | async-start | bytes 2621440 | tf_op jit(solution)/shard_map/all_gather | solution.py:35
  13.4 181.8 %reduce-scatter.10.cloned.1.call-start = ((), (), s32[]{:S(2)}) async-start(), calls=%async_computation.8 | async-start | bytes 589824
  142.3 4.8 %copy-start.1 = (bf16[16,64,4,64]{1,3,2,0:T(8,128)(2,1)S(1)}, bf16[16,64,4,64]{1,3,2,0:T(8,128)(2,1)}, u32[]{:S(2)}) copy-start(bf16[16,64,4,64]{1,3,2,0:T(8,128)(2,1)} %copy.48) | copy-start | bytes 1572868
  147.1 3.4 %copy-start.10 = (f32[16,4,64,64]{2,3,1,0:T(8,128)S(1)}, f32[16,4,64,64]{2,3,1,0:T(8,128)}, u32[]{:S(2)}) copy-start(f32[16,4,64,64]{2,3,1,0:T(8,128)} %get-tuple-element.17) | copy-start | bytes 3145732
  158.5 3.8 %copy-start.3 = (bf16[16,64,4,1,64]{4,3,2,1,0:T(2,128)(2,1)S(1)}, bf16[16,64,4,1,64]{4,3,2,1,0:T(2,128)(2,1)}, u32[]{:S(2)}) copy-start(bf16[16,64,4,1,64]{4,3,2,1,0:T(2,128)(2,1)} %get-tuple-element.12) | copy-start | bytes 1572868
  162.1 5.8 %copy-start.5 = (bf16[16,64,4,1,64]{1,4,2,0,3:T(8,128)(2,1)S(1)}, bf16[16,64,4,1,64]{1,4,2,0,3:T(8,128)(2,1)}, u32[]{:S(2)}) copy-start(bf16[16,64,4,1,64]{1,4,2,0,3:T(8,128)(2,1)} %fusion.25) | copy-start | bytes 1572868
  162.1 74.6 %reduce-scatter.8.cloned.1.call-start = ((), (), s32[]{:S(2)}) async-start(), calls=%async_computation.7 | async-start | bytes 1769472 | tf_op jit(solution)/shard_map/reduce_scatter | solution.py:91
  175.9 5.3 %copy-start.4 = (bf16[1024,768]{0,1:T(8,128)(2,1)S(1)}, bf16[1024,768]{0,1:T(8,128)(2,1)}, u32[]{:S(2)}) copy-start(bf16[1024,768]{0,1:T(8,128)(2,1)} %reshape.99) | copy-start | bytes 4718596
  175.9 5.3 %copy-start.9 = (bf16[1024,768]{1,0:T(8,128)(2,1)S(1)}, bf16[1024,768]{1,0:T(8,128)(2,1)}, u32[]{:S(2)}) copy-start(bf16[1024,768]{1,0:T(8,128)(2,1)} %all-gather.6.cloned.1.call-done) | copy-start | bytes 4718596
  181.1 101.4 %reduce-scatter.6.cloned.1.call-start = ((), (), s32[]{:S(2)}) async-start(), calls=%async_computation.6 | async-start | bytes 2621440 | tf_op jit(solution)/shard_map/reduce_scatter | solution.py:94
  184.3 98.2 %copy-start = (bf16[256,1024]{1,0:T(8,128)(2,1)S(1)}, bf16[256,1024]{1,0:T(8,128)(2,1)}, u32[]{:S(2)}) copy-start(bf16[256,1024]{1,0:T(8,128)(2,1)} %param.7) | copy-start | bytes 1572868
  184.4 98.2 %copy-start.7 = (f32[1024]{0:T(1024)S(1)}, f32[1024]{0:T(1024)}, u32[]{:S(2)}) copy-start(f32[1024]{0:T(1024)} %param.10) | copy-start | bytes 12292
  184.4 139.3 %copy-start.2 = (bf16[256,1024]{1,0:T(8,128)(2,1)S(1)}, bf16[256,1024]{1,0:T(8,128)(2,1)}, u32[]{:S(2)}) copy-start(bf16[256,1024]{1,0:T(8,128)(2,1)} %param.8) | copy-start | bytes 1572868
Sparse Core Ops, SparseCore 0:
  9.9 28.9 all-gather.5
  41.0 45.6 all-gather.3
  88.3 44.4 all-gather.7
  162.2 32.9 reduce-scatter.9
  198.3 38.3 reduce-scatter.7
  238.8 43.6 reduce-scatter.5
where the time goes:
time: 333 us
  waiting for transfers between devices  182 us (55%)
  blocking collectives  52.1 us (16%)
  matrix products  41.2 us (12%)
  local copies, waits for them, and re-layouts  29 us (9%)
  between operations  14.3 us (4%)
  other arithmetic  13.4 us (4%)
    all_gather x1, waiting for transfers between devices, on_device(): all_normed = lax.all_gather(normed, 'tensor', axis=0, tiled=True)  47.8 us
    reduce_scatter x1, waiting for transfers between devices, on_device(): lax.psum_scatter(lax.dot_general(grad_proj, qkv_cols, (((1,), (1,)), ((),...  44.1 us
    reduce_scatter x1, waiting for transfers between devices, on_device(): lax.psum_scatter(qkv_part.astype(jnp.bfloat16), 'dp', scatter_dimension=0...  39.9 us
    psum x1, blocking collectives, on_device(): lax.psum((jnp.sum(grad_normed * scaled, axis=0), jnp.sum(grad_normed, axi...  39.5 us
    all_gather x1, waiting for transfers between devices, on_device(): all_upstream = lax.all_gather(upstream, 'tensor', axis=0, tiled=True)  25.9 us
    all_gather x1, waiting for transfers between devices, on_device(): qkv_cols = lax.all_gather(w_qkv, 'dp', axis=0, tiled=True)  12.7 us
    all_gather x1, blocking collectives, on_device(): out_rows = lax.all_gather(w_out, 'dp', axis=1, tiled=True)  12.6 us
    unnamed x7, waiting for transfers between devices  12 us
  transfers between devices with their start and end apart: 6, of which 6 were waited for; matrix products, arithmetic and copies ran while one was open for 15% of the time, Pallas kernels for 0%

commit v1 on v0

--- a/solution.py
+++ b/solution.py
@@ -29,7 +29,18 @@
         .astype(jnp.float32)
     )
     normed, scaled, inverse_std = layer_norm(tokens, norm_gain, norm_bias)
-    all_normed = lax.all_gather(normed, "tensor", axis=0, tiled=True)
+    total_devices = lax.axis_size("tensor")
+    w1 = [(b - 1, b) for b in range(1, total_devices)] + [(total_devices - 1, 0)]
+    work_now = normed
+    bank = [work_now]
+    dev_j = 0
+    while dev_j < total_devices - 1:
+        work_now = lax.ppermute(work_now, "tensor", perm=w1)
+        bank += [work_now]
+        dev_j = dev_j + 1
+    all_values = jnp.concatenate([*reversed(bank)], axis=0)
+    then = lax.axis_index("tensor")
+    all_normed = jnp.roll(all_values, (then + 1) * work_now.shape[0], axis=0)
     qkv_cols = lax.all_gather(w_qkv, "dp", axis=0, tiled=True)
     out_rows = lax.all_gather(w_out, "dp", axis=1, tiled=True)
     all_upstream = lax.all_gather(upstream, "tensor", axis=0, tiled=True)

time: 333 us -> 290 us (0.87)
  waiting for transfers between devices: 182 us -> 122 us
  local copies, waits for them, and re-layouts: 29 us -> 42.2 us
    all_gather x1 -> x0, waiting for transfers between devices: 47.8 us -> none  [on_device(): all_normed = lax.all_gather(normed, 'tensor', axis=0, tiled=True)]
    ppermute x0 -> x3, waiting for transfers between devices: none -> 32.5 us  [on_device(): work_now = lax.ppermute(work_now, 'tensor', perm=w1)]
    all_gather x1, waiting for transfers between devices: 25.9 us -> 0.02 us  [on_device(): all_upstream = lax.all_gather(upstream, 'tensor', axis=0, tiled=True)]
    all_gather x1, waiting for transfers between devices: 12.7 us -> 0.01 us  [on_device(): qkv_cols = lax.all_gather(w_qkv, 'dp', axis=0, tiled=True)]
    unnamed x7 -> x6, waiting for transfers between devices: 12 us -> 5.52 us
    unnamed x24 -> x28, local copies, waits for them, and re-layouts: 1.99 us -> 8.12 us
  transfers between devices with their start and end apart: 6 -> 8, of which waited for: 6 -> 6; matrix products, arithmetic and copies ran while one was open for 15% -> 25% of each run, Pallas kernels for 0% -> 0%
where the time goes in v1:
time: 290 us; the launch traced here: 289 us
  waiting for transfers between devices  122 us (42%)
  blocking collectives  50.3 us (17%)
  local copies, waits for them, and re-layouts  42.2 us (15%)
  matrix products  42.2 us (15%)
  other arithmetic  15.1 us (5%)
  between operations  13.9 us (5%)
  starting transfers between devices  3.53 us (1%)
    reduce_scatter x1, waiting for transfers between devices, on_device(): lax.psum_scatter(lax.dot_general(grad_proj, qkv_cols, (((1,), (1,)), ((),...  44.1 us
    reduce_scatter x1, waiting for transfers between devices, on_device(): lax.psum_scatter(qkv_part.astype(jnp.bfloat16), 'dp', scatter_dimension=0...  39.9 us
    psum x1, blocking collectives, on_device(): lax.psum((jnp.sum(grad_normed * scaled, axis=0), jnp.sum(grad_normed, axi...  39.5 us
    ppermute x3, waiting for transfers between devices, on_device(): work_now = lax.ppermute(work_now, 'tensor', perm=w1)  32.5 us
    slice x1, local copies, waits for them, and re-layouts, on_device(): value_rows = projected[:, :, :, 2]  11.3 us
    all_gather x1, blocking collectives, on_device(): out_rows = lax.all_gather(w_out, 'dp', axis=1, tiled=True)  10.8 us
    unnamed x28, local copies, waits for them, and re-layouts  8.12 us
  transfers between devices with their start and end apart: 8, of which 6 were waited for; matrix products, arithmetic and copies ran while one was open for 25% of the time, Pallas kernels for 0%

profile of v1, /device:TPU:0, one launch (start us, length us, event | category | flops | bytes accessed | tf_op | source)
XLA Modules:
  0.0 289.4 jit_solution(14829815670892496258)
XLA Ops:
  11.9 3.1 %collective-permute-start = (bf16[256,1024]{1,0:T(8,128)(2,1)S(1)}, bf16[256,1024]{1,0:T(8,128)(2,1)S(1)}, u32[]{:S(2)}, u32[]{:S(2)}) collective-permute-start(bf16[256,1024]{1,0:T(8,128)(2,1)S(1)} %fusion.54), channel_id=1, source_target_pairs={{0,1},{1,2},{2,3},{3,0},{4,5},{5,6},{6,7},{7,4},{8,9},{9,10},{10,1... | collective-permute-start | bytes 1572872 | tf_op jit(solution)/shard_map/ppermute | solution.py:38
  15.0 13.9 %collective-permute-done = bf16[256,1024]{1,0:T(8,128)(2,1)S(1)} collective-permute-done((bf16[256,1024]{1,0:T(8,128)(2,1)S(1)}, bf16[256,1024]{1,0:T(8,128)(2,1)S(1)}, u32[]{:S(2)}, u32[]{:S(2)}) %collective-permute-start) | collective-permute-done | bytes 524320 | tf_op jit(solution)/shard_map/ppermute | solution.py:38
  28.9 14.9 %collective-permute-done.1 = bf16[256,1024]{1,0:T(8,128)(2,1)S(1)} collective-permute-done((bf16[256,1024]{1,0:T(8,128)(2,1)S(1)}, bf16[256,1024]{1,0:T(8,128)(2,1)S(1)}, u32[]{:S(2)}, u32[]{:S(2)}) %collective-permute-start.1) | collective-permute-done | bytes 524320 | tf_op jit(solution)/shard_map/ppermute | solution.py:38
  44.1 10.8 %all_gather.11 = bf16[256,1024]{1,0:T(8,128)(2,1)} all-gather(bf16[256,128]{1,0:T(8,128)(2,1)S(1)} %copy-done.6), channel_id=1, replica_groups=mesh['dp'=8,'tensor'=4] {'dp'}, dimensions={1}, use_global_device_ids=true | all-gather | bytes 589824 | tf_op jit(solution)/shard_map/all_gather | solution.py:45
  54.9 3.7 %collective-permute-done.2 = bf16[256,1024]{1,0:T(8,128)(2,1)S(1)} collective-permute-done((bf16[256,1024]{1,0:T(8,128)(2,1)S(1)}, bf16[256,1024]{1,0:T(8,128)(2,1)S(1)}, u32[]{:S(2)}, u32[]{:S(2)}) %collective-permute-start.2) | collective-permute-done | bytes 524320 | tf_op jit(solution)/shard_map/ppermute | solution.py:38
  65.8 3.8 %fusion.14 = bf16[1024,768]{1,0:T(8,128)(2,1)S(1)} fusion(bf16[1024,768]{1,0:T(8,128)(2,1)} %all-gather.3.cloned.1.call-done, bf16[2048,1024]{1,0:T(8,128)(2,1)} %constant_dynamic-update-slice_fusion, s32[]{:T(128)S(6)} %select_n.22), kind=kOutput, calls=%fused_computation.18 | convolution fusion | flops 1611399168 | bytes 5242884 | tf_op jit(solution)/shard_map/dot_general | solution.py:53
  69.7 5.2 %reshape.105 = bf16[16,64,4,3,64]{4,3,2,1,0:T(4,128)(2,1)} reshape(bf16[1024,768]{1,0:T(8,128)(2,1)S(1)} %fusion.14) | data formatting | bytes 3145728 | tf_op jit(solution)/shard_map/reshape | solution.py:56
  74.8 11.3 %fusion.83 = (bf16[16,64,4,1,64]{4,3,2,1,0:T(2,128)(2,1)S(1)}, bf16[16,64,4,1,64]{4,3,2,1,0:T(2,128)(2,1)}, bf16[16,64,4,1,64]{4,3,2,1,0:T(2,128)(2,1)}) fusion(bf16[16,64,4,3,64]{4,3,2,1,0:T(4,128)(2,1)} %reshape.105), kind=kLoop, calls=%fused_computation.92 | loop fusion | bytes 3145728 | tf_op jit(solution)/shard_map/slice | solution.py:59
  86.2 4.7 %fusion.84 = (f32[16,4,64]{2,1,0:T(4,128)S(1)}, f32[16,4,64,64]{2,3,1,0:T(8,128)}) fusion(pred[16,64]{1,0:T(8,128)(4,1)S(1)} %get-tuple-element.14, bf16[16,64,4,1,64]{4,3,2,1,0:T(2,128)(2,1)} %get-tuple-element.13, bf16[16,64,4,1,64]{4,3,2,1,0:T(2,128)(2,1)} %get-tuple-element.12), kind=kOutput, calls=%fused_computation.93 | convolution fusion | flops 34603072 | bytes 2114560 | tf_op jit(solution)/shard_map/sub | solution.py:66
  96.6 3.2 %fusion.43 = bf16[1024,256]{1,0:T(8,128)(2,1)} fusion(bf16[256,1024]{1,0:T(8,128)(2,1)} %all_gather.11, bf16[1024,1024]{1,0:T(8,128)(2,1)} %all-gather.5.cloned.1.call-done, bf16[1024]{0:T(1024)(128)(2,1)S(1)} %reshape.102), kind=kOutput, calls=%fused_computation.38 | convolution fusion | flops 538181632 | bytes 3147776 | tf_op jit(solution)/shard_map/dot_general | solution.py:78
  99.9 2.8 reshape.98
  104.9 3.1 %fusion.72 = f32[16,4,64,64]{2,3,1,0:T(8,128)} fusion(bf16[16,64,4,64]{1,3,2,0:T(8,128)(2,1)} %copy.48, bf16[16,64,4,1,64]{4,3,2,1,0:T(2,128)(2,1)S(1)} %get-tuple-element.11), kind=kOutput, calls=%fused_computation.67 | convolution fusion | flops 33554432 | bytes 2097152 | tf_op jit(solution)/shard_map/bqhe,bkhe->bhqk/dot_general | solution.py:82
  109.7 5.5 %fusion.40 = bf16[16,64,4,1,64]{1,4,2,0,3:T(8,128)(2,1)} fusion(f32[16,4,64,64]{2,3,1,0:T(8,128)} %fusion.72, bf16[16,64,4,1,64]{4,3,2,1,0:T(2,128)(2,1)S(1)} %copy-done.4, f32[16,4,64,64]{2,3,1,0:T(8,128)} %get-tuple-element.17, f32[16,4,64]{2,1,0:T(4,128)S(1)} %get-tuple-element.16), kind=kOutput, calls=%fused_computation.35 | convolution fusion | flops 35655744 | bytes 3162112 | tf_op jit(solution)/shard_map/bhqk,bkhe->bqhe/dot_general | solution.py:90
  115.2 3.3 %fusion.46 = bf16[256,1024]{1,0:T(8,128)(2,1)} fusion(bf16[1024,256]{0,1:T(8,128)(2,1)S(1)} %reshape.100, bf16[1024,1024]{1,0:T(8,128)(2,1)} %all-gather.5.cloned.1.call-done, bf16[1024]{0:T(1024)(128)(2,1)S(1)} %reshape.102), kind=kOutput, calls=%fused_computation.39 | convolution fusion | flops 538181632 | bytes 3147776 | tf_op jit(solution)/shard_map/dot_general | solution.py:72
  120.9 5.5 %fusion.37 = bf16[16,64,4,1,64]{1,4,2,0,3:T(8,128)(2,1)} fusion(f32[16,4,64,64]{2,3,1,0:T(8,128)} %fusion.72, bf16[16,64,4,1,64]{4,3,2,1,0:T(2,128)(2,1)S(1)} %copy-done.3, f32[16,4,64,64]{2,3,1,0:T(8,128)} %get-tuple-element.17, f32[16,4,64]{2,1,0:T(4,128)S(1)} %get-tuple-element.16), kind=kOutput, calls=%fused_computation.34 | convolution fusion | flops 35655744 | bytes 3162112 | tf_op jit(solution)/shard_map/bhqk,bqhe->bkhe/dot_general | solution.py:93
  126.5 2.7 pad_maximum_fusion
  129.1 4.2 %copy.50 = bf16[16,64,4,3,64]{1,0,4,3,2:T(8,128)(2,1)} copy(bf16[16,64,4,3,64]{1,4,2,0,3:T(8,128)(2,1)S(1)} %pad_maximum_fusion) | data formatting | bytes 3145728 | tf_op jit(solution)/shard_map/stack | solution.py:96
  133.3 4.5 %reshape.99 = bf16[1024,768]{0,1:T(8,128)(2,1)S(1)} reshape(bf16[16,64,4,3,64]{1,0,4,3,2:T(8,128)(2,1)} %copy.50) | data formatting | bytes 3145728 | tf_op jit(solution)/shard_map/reshape | solution.py:96
  137.8 4.6 %fusion.17 = bf16[1024,768]{1,0:T(8,128)(2,1)} fusion(bf16[1024,768]{0,1:T(8,128)(2,1)S(1)} %reshape.99, bf16[2048,1024]{1,0:T(8,128)(2,1)} %constant_dynamic-update-slice_fusion, s32[]{:T(128)S(6)} %select_n.22), kind=kOutput, calls=%fused_computation.19 | convolution fusion | flops 1611399168 | bytes 5242884 | tf_op jit(solution)/shard_map/dot_general | solution.py:99
  142.5 4.6 %convolution_convert_fusion = bf16[1024,1024]{1,0:T(8,128)(2,1)} fusion(bf16[1024,768]{0,1:T(8,128)(2,1)S(1)} %reshape.99, bf16[1024,768]{1,0:T(8,128)(2,1)} %all-gather.3.cloned.1.call-done), kind=kOutput, calls=%fused_computation.8 | convolution fusion | flops 1611661312 | bytes 5242880 | tf_op jit(solution)/shard_map/dot_general | solution.py:106
  147.3 4.8 %reduce-scatter.10.cloned.1.call-done = bf16[128,256]{1,0:T(8,128)(2,1)} async-done(((bf16[1024,256]{1,0:T(8,128)(2,1)}), bf16[128,256]{1,0:T(8,128)(2,1)}) %reduce-scatter.10.cloned.1.call-update) | async-done | bytes 65552
  153.7 39.9 %reduce-scatter.8.cloned.1.call-done = bf16[128,768]{1,0:T(8,128)(2,1)} async-done(((bf16[1024,768]{1,0:T(8,128)(2,1)}), bf16[128,768]{1,0:T(8,128)(2,1)}) %reduce-scatter.8.cloned.1.call-update) | async-done | bytes 196624 | tf_op jit(solution)/shard_map/reduce_scatter | solution.py:102
  195.3 44.1 %reduce-scatter.6.cloned.1.call-done = bf16[256,1024]{1,0:T(8,128)(2,1)} async-done(((bf16[1024,1024]{1,0:T(8,128)(2,1)}), bf16[256,1024]{1,0:T(8,128)(2,1)}) %reduce-scatter.6.cloned.1.call-update) | async-done | bytes 524304 | tf_op jit(solution)/shard_map/reduce_scatter | solution.py:105
  241.0 39.5 %all-reduce = (f32[1024]{0:T(1024)}, f32[1024]{0:T(1024)}) all-reduce(f32[1024]{0:T(1024)S(1)} %get-tuple-element.5, f32[1024]{0:T(1024)S(1)} %get-tuple-element.8), channel_id=1, replica_groups=mesh['dp'=8,'tensor'=4] {'dp','tensor'}, use_global_device_ids=true, to_apply=%region_11.12 | all-reduce | flops 2048 | bytes 16384 | tf_op jit(solution)/shard_map/psum | solution.py:113
  (64 shorter events, 31.7 us)
Async XLA Ops:
  7.2 36.7 %copy-start.8 = (s32[16]{0:T(128)S(1)}, s32[16]{0:T(128)}, u32[]{:S(2)}) copy-start(s32[16]{0:T(128)} %param.9) | copy-start | bytes 196
  7.2 36.9 %copy-start.6 = (bf16[256,128]{1,0:T(8,128)(2,1)S(1)}, bf16[256,128]{1,0:T(8,128)(2,1)}, u32[]{:S(2)}) copy-start(bf16[256,128]{1,0:T(8,128)(2,1)} %param.13) | copy-start | bytes 196612
  7.2 58.6 %all-gather.3.cloned.1.call-start = ((), (), s32[]{:S(2)}) async-start(), calls=%async_computation.3 | async-start | bytes 1769472 | tf_op jit(solution)/shard_map/all_gather | solution.py:44
  7.9 88.7 %all-gather.5.cloned.1.call-start = ((), (), s32[]{:S(2)}) async-start(), calls=%async_computation.4 | async-start | bytes 2621440 | tf_op jit(solution)/shard_map/all_gather | solution.py:46
  11.8 49.3 %copy-start = (bf16[256,1024]{1,0:T(8,128)(2,1)S(1)}, bf16[256,1024]{1,0:T(8,128)(2,1)}, u32[]{:S(2)}) copy-start(bf16[256,1024]{1,0:T(8,128)(2,1)} %param.7) | copy-start | bytes 1572868
  11.9 49.3 %copy-start.5 = (f32[1024]{0:T(1024)S(1)}, f32[1024]{0:T(1024)}, u32[]{:S(2)}) copy-start(f32[1024]{0:T(1024)} %param.10) | copy-start | bytes 12292
  11.9 49.3 %copy-start.7 = (f32[1024]{0:T(1024)S(1)}, f32[1024]{0:T(1024)}, u32[]{:S(2)}) copy-start(f32[1024]{0:T(1024)} %param.11) | copy-start | bytes 12292
  11.9 17.1 %collective-permute-start = (bf16[256,1024]{1,0:T(8,128)(2,1)S(1)}, bf16[256,1024]{1,0:T(8,128)(2,1)S(1)}, u32[]{:S(2)}, u32[]{:S(2)}) collective-permute-start(bf16[256,1024]{1,0:T(8,128)(2,1)S(1)} %fusion.54), channel_id=1, source_target_pairs={{0,1},{1,2},{2,3},{3,0},{4,5},{5,6},{6,7},{7,4},{8,9},{9,10},{10,1... | collective-permute-start | bytes 1572872 | tf_op jit(solution)/shard_map/ppermute | solution.py:38
  28.9 14.9 %collective-permute-start.1 = (bf16[256,1024]{1,0:T(8,128)(2,1)S(1)}, bf16[256,1024]{1,0:T(8,128)(2,1)S(1)}, u32[]{:S(2)}, u32[]{:S(2)}) collective-permute-start(bf16[256,1024]{1,0:T(8,128)(2,1)S(1)} %collective-permute-done), channel_id=1, source_target_pairs={{0,1},{1,2},{2,3},{3,0},{4,5},{5,6},{6,7},{7,4},{8,9},{9,10},{10,1... | collective-permute-start | bytes 1572872 | tf_op jit(solution)/shard_map/ppermute | solution.py:38
  43.8 14.8 %collective-permute-start.2 = (bf16[256,1024]{1,0:T(8,128)(2,1)S(1)}, bf16[256,1024]{1,0:T(8,128)(2,1)S(1)}, u32[]{:S(2)}, u32[]{:S(2)}) collective-permute-start(bf16[256,1024]{1,0:T(8,128)(2,1)S(1)} %collective-permute-done.1), channel_id=1, source_target_pairs={{0,1},{1,2},{2,3},{3,0},{4,5},{5,6},{6,7},{7,4},{8,9},{9,10},{10,1... | collective-permute-start | bytes 1572872 | tf_op jit(solution)/shard_map/ppermute | solution.py:38
  43.8 108.3 %reduce-scatter.10.cloned.1.call-start = ((), (), s32[]{:S(2)}) async-start(), calls=%async_computation.7 | async-start | bytes 589824
  104.9 3.1 %copy-start.1 = (bf16[16,64,4,64]{1,3,2,0:T(8,128)(2,1)S(1)}, bf16[16,64,4,64]{1,3,2,0:T(8,128)(2,1)}, u32[]{:S(2)}) copy-start(bf16[16,64,4,64]{1,3,2,0:T(8,128)(2,1)} %copy.48) | copy-start | bytes 1572868
  104.9 3.1 %copy-start.9 = (f32[16,4,64,64]{2,3,1,0:T(8,128)S(1)}, f32[16,4,64,64]{2,3,1,0:T(8,128)}, u32[]{:S(2)}) copy-start(f32[16,4,64,64]{2,3,1,0:T(8,128)} %get-tuple-element.17) | copy-start | bytes 3145732
  108.0 1.7 copy-start.4
  115.2 5.7 %copy-start.3 = (bf16[16,64,4,1,64]{4,3,2,1,0:T(2,128)(2,1)S(1)}, bf16[16,64,4,1,64]{4,3,2,1,0:T(2,128)(2,1)}, u32[]{:S(2)}) copy-start(bf16[16,64,4,1,64]{4,3,2,1,0:T(2,128)(2,1)} %get-tuple-element.12) | copy-start | bytes 1572868
  120.7 73.0 %reduce-scatter.8.cloned.1.call-start = ((), (), s32[]{:S(2)}) async-start(), calls=%async_computation.6 | async-start | bytes 1769472 | tf_op jit(solution)/shard_map/reduce_scatter | solution.py:102
  142.4 97.0 %reduce-scatter.6.cloned.1.call-start = ((), (), s32[]{:S(2)}) async-start(), calls=%async_computation.5 | async-start | bytes 2621440 | tf_op jit(solution)/shard_map/reduce_scatter | solution.py:105
  147.1 133.5 %copy-start.2 = (bf16[256,1024]{1,0:T(8,128)(2,1)S(1)}, bf16[256,1024]{1,0:T(8,128)(2,1)}, u32[]{:S(2)}) copy-start(bf16[256,1024]{1,0:T(8,128)(2,1)} %param.8) | copy-start | bytes 1572868
Sparse Core Ops, SparseCore 0:
  9.9 28.2 all-gather.2
  44.0 48.4 all-gather.4
  120.8 31.2 reduce-scatter.9
  155.3 38.3 reduce-scatter.7
  195.8 43.6 reduce-scatter.5
